TPU v7x, 256 devices: a whole 4x4x8 slice. The times are simulated.
256 devices in a mesh: grp: 16 (over x, z_lo, core), dev: 16 (over z_hi, y).
Axes of the slice: x: 4, y: 4, z: 8 (z_hi: 4, z_lo: 2; z = z_hi * 2 + z_lo), core: 2. Of those that a mesh axis runs over, the one named last changes fastest.
Arguments:
- a_tiles: float32 [8192, 3, 128, 128], P(('grp', 'dev')), may hold values from -1.7071068 to 18.707107
- prolong: float32 [8192, 2, 128, 128], P(('grp', 'dev')), may hold values from -0.5 to 0.5
- coarse_ids: int32 [8192, 2], P(('grp', 'dev')), may hold values from 0 to 3, as said below
Outputs:
- coarse: float32 [8192, 1536], P(('grp', 'dev'))
Inputs may be any that keep to these rules, and one draw needn't show every extreme that they name: `coarse_ids`: each fine block names 2 different coarse tiles, numbered within its own group.
All inputs are finite; a program needn't handle non-finite values.
Results may differ from a plain program's by a relative error of at most 0.0001.
Values sent between devices are 32-bit elements; how exact they have to be, the bound alone decides.
A program may use at most 128 MiB of HBM per device.

v0:
```python
import jax
import jax.numpy as jnp
from jax import lax
from jax.sharding import Mesh
from jax.sharding import PartitionSpec as P

COARSE_DEV = 32
DEV = ("dev_0", "dev_1")
GRP = ("grp_0", "grp_1", "grp_2")
GRP_DEV = ("grp_0", "grp_1", "grp_2", "dev_0", "dev_1")


def with_halo(x, sides, width):
    edges = {}
    for axis, dim in sides:
        peers, length = (lax.axis_size(axis), x.shape[dim])
        up = [(i, (i + 1) % peers) for i in range(peers)]
        last = lax.slice_in_dim(x, length - width, length, axis=dim)
        first = lax.slice_in_dim(x, 0, width, axis=dim)
        edges[dim] = (
            lax.ppermute(last, axis, up),
            lax.ppermute(first, axis, [(b, a) for a, b in up]),
        )
    done = []
    for _, dim in sides:
        low, high = edges[dim]
        around = [(width, width) if d in done else (0, 0) for d in range(x.ndim)]
        x = jnp.concatenate([jnp.pad(low, around), x, jnp.pad(high, around)], axis=dim)
        done.append(dim)
    return x


def by_axis(x, axes):
    for axis in axes:
        x = lax.psum(x, axis)
    return x


def cut_along(x, dim, peers):
    dims = x.shape
    pieces = x.reshape(*dims[:dim], peers, dims[dim] // peers, *dims[dim + 1 :])
    return jnp.moveaxis(pieces, dim, 0)


def sum_at_owner(x, axis, dim):
    peers = lax.axis_size(axis)
    pieces = lax.all_to_all(cut_along(x, dim, peers), axis, 0, 0, tiled=True)
    return jnp.sum(pieces, axis=0)


def coarse_tiles(own_a, nearby):
    block_count = own_a.shape[0]
    slot_count = nearby.shape[1]
    tile_size = nearby.shape[2]
    widened = jnp.transpose(nearby, (0, 2, 1, 3)).reshape(
        block_count + 2, tile_size, slot_count * tile_size
    )
    stacked = jnp.stack([widened[:-2], widened[1:-1], widened[2:]], axis=1)
    right_prod = jnp.einsum("bnij,bnjk->bnik", own_a, stacked, precision=lax.Precision.HIGHEST)
    right_prod = jnp.transpose(right_prod, (0, 2, 1, 3)).reshape(
        block_count, tile_size, 3 * slot_count * tile_size
    )
    left_prod = jnp.einsum(
        "bik,bic->bkc", widened[1:-1], right_prod, precision=lax.Precision.HIGHEST
    )
    left_prod = left_prod.reshape(block_count, slot_count, tile_size, 3 * slot_count, tile_size)
    return jnp.transpose(left_prod, (0, 1, 3, 2, 4))


def local(a_tiles, prolong, coarse_ids):
    fine_count = a_tiles.shape[0]
    tile_size = a_tiles.shape[-1]
    dev_count = lax.axis_size(DEV)
    grp_count = lax.axis_size(GRP)
    dev_index = lax.axis_index(DEV)
    coarse_grp = COARSE_DEV * dev_count
    ctiles = coarse_grp // tile_size
    nearby, nearby_ids = (
        with_halo(prolong, ((GRP_DEV, 0),), 1),
        with_halo(coarse_ids, ((GRP_DEV, 0),), 1),
    )
    position = jnp.arange(fine_count, dtype=jnp.int32)
    lower_win = jnp.where((position == 0) & (dev_index == 0), 0, 1).astype(jnp.int32)
    upper_win = jnp.where((position == fine_count - 1) & (dev_index == dev_count - 1), 2, 1).astype(
        jnp.int32
    )
    col_tiles = jnp.concatenate(
        [
            lower_win[:, None] * ctiles + nearby_ids[:-2],
            ctiles + coarse_ids,
            upper_win[:, None] * ctiles + nearby_ids[2:],
        ],
        axis=1,
    )
    products = coarse_tiles(a_tiles, nearby)
    partial_value = jnp.zeros((ctiles, 3 * ctiles, tile_size, tile_size), jnp.float32)
    partial_value = partial_value.at[coarse_ids[:, :, None], col_tiles[:, None, :]].add(products)
    partial_rows = jnp.transpose(partial_value, (0, 2, 1, 3)).reshape(coarse_grp, 3 * coarse_grp)
    own_trace = jnp.sum(jnp.diagonal(partial_rows[:, coarse_grp : 2 * coarse_grp]))
    trace_sum = by_axis(own_trace, GRP_DEV)
    middle_rows = sum_at_owner(partial_rows[:, coarse_grp : 2 * coarse_grp], DEV, 0)
    at_first = dev_index == 0
    at_last = dev_index == dev_count - 1
    edge_block = jnp.where(
        at_first,
        partial_rows[:, :coarse_grp],
        jnp.where(at_last, partial_rows[:, 2 * coarse_grp :], 0.0),
    )
    received = lax.all_to_all(edge_block, DEV, split_axis=0, concat_axis=0, tiled=True)
    lower_rows = received[:COARSE_DEV]
    upper_rows = received[(dev_count - 1) * COARSE_DEV :]
    owned_rows = jnp.concatenate([lower_rows, middle_rows, upper_rows], axis=1)
    mean_diag = trace_sum / (grp_count * coarse_grp)
    return owned_rows / mean_diag


def solution(mesh):
    torus = Mesh(mesh.devices.reshape(4, 2, 2, 4, 4), ("grp_0", "grp_1", "grp_2", "dev_0", "dev_1"))
    return jax.shard_map(
        local,
        mesh=torus,
        in_specs=(P(GRP_DEV, None, None, None), P(GRP_DEV, None, None, None), P(GRP_DEV, None)),
        out_specs=P(GRP_DEV, None),
        check_vma=False,
    )
```

profile of v0, /device:TPU:32, one launch (start us, length us, event | category | flops | bytes accessed | tf_op | source)
XLA Modules:
  0.0 308.0 jit_solution(531776822477899482)
XLA Ops:
  2.4 6.2 %collective-permute-start.1 = (s32[1,2]{0,1:T(2,128)S(1)}, s32[1,2]{0,1:T(2,128)S(1)}, u32[]{:S(2)}, u32[]{:S(2)}) collective-permute-start(s32[1,2]{0,1:T(2,128)S(1)} %get-tuple-element.19), channel_id=1, source_target_pairs={{1,0},{2,1},{3,2},{4,3},{5,4},{6,5},{7,6},{8,7},{9,8},{10,9},{11,1... | collective-permute-start | bytes 32 | tf_op jit(solution)/shard_map/ppermute | solution.py:22
  9.7 6.9 %collective-permute-start.3 = (f32[1,2,128,128]{3,2,1,0:T(8,128)S(1)}, f32[1,2,128,128]{3,2,1,0:T(8,128)S(1)}, u32[]{:S(2)}, u32[]{:S(2)}) collective-permute-start(f32[1,2,128,128]{3,2,1,0:T(8,128)S(1)} %get-tuple-element.9), channel_id=1, source_target_pairs={{1,0},{2,1},{3,2},{4,3},{5,4},{6,5},{7,6},{8,7},{9,8},{10,9},{11,1... | collective-permute-start | bytes 393224 | tf_op jit(solution)/shard_map/ppermute | solution.py:22
  19.5 3.2 %collective-permute-done.2 = f32[1,2,128,128]{3,2,1,0:T(8,128)S(1)} collective-permute-done((f32[1,2,128,128]{3,2,1,0:T(8,128)S(1)}, f32[1,2,128,128]{3,2,1,0:T(8,128)S(1)}, u32[]{:S(2)}, u32[]{:S(2)}) %collective-permute-start.2) | collective-permute-done | bytes 131104 | tf_op jit(solution)/shard_map/ppermute | solution.py:21
  22.8 2.5 maximum_bitcast_fusion
  25.3 4.7 %fusion.10 = (f32[32,128,2,128]{3,1,2,0:T(8,128)}, f32[32,128,2,128]{3,1,2,0:T(8,128)}, f32[32,128,2,128]{3,1,2,0:T(8,128)}) fusion(f32[34,128,2,128]{3,1,2,0:T(8,128)S(1)} %maximum_bitcast_fusion), kind=kLoop, calls=%fused_computation.33 | loop fusion | bytes 25165824 | tf_op jit(solution)/shard_map/slice | solution.py:58
  30.0 5.6 %copy.31 = f32[32,128,2,128]{1,3,2,0:T(8,128)} copy(f32[32,128,2,128]{3,1,2,0:T(8,128)} %get-tuple-element.7) | data formatting | bytes 8388608 | tf_op jit(solution)/shard_map/slice | solution.py:64
  35.6 5.6 %copy.32 = f32[32,128,2,128]{1,3,2,0:T(8,128)} copy(f32[32,128,2,128]{3,1,2,0:T(8,128)} %get-tuple-element.5) | data formatting | bytes 8388608 | tf_op jit(solution)/shard_map/slice | solution.py:58
  41.2 5.6 %copy.34 = f32[32,128,2,128]{1,3,2,0:T(8,128)} copy(f32[32,128,2,128]{3,1,2,0:T(8,128)} %get-tuple-element.6) | data formatting | bytes 8388608 | tf_op jit(solution)/shard_map/slice | solution.py:58
  46.8 15.3 %fusion = f32[32,3,256,128]{3,2,1,0:T(8,128)S(1)} fusion(f32[32,3,128,128]{3,2,1,0:T(8,128)} %param.3, f32[32,1,128,256]{2,3,1,0:T(8,128)} %bitcast.41, f32[32,1,128,256]{2,3,1,0:T(8,128)} %bitcast.37, f32[32,1,128,256]{2,3,1,0:T(8,128)} %bitcast.40), kind=kOutput, calls=%fused_computation.2 | convolution fusion | flops 4838129664 | bytes 31457280 | tf_op jit(solution)/shard_map/bnij,bnjk->bnik/dot_general | solution.py:59
  62.2 23.4 %fusion.14 = f32[32,256,768]{1,2,0:T(8,128)} fusion(f32[32,128,256]{1,2,0:T(8,128)S(1)} %bitcast.38, f32[32,128,768]{1,2,0:T(8,128)S(1)} %bitcast.35), kind=kOutput, calls=%fused_computation.37 | convolution fusion | flops 9663676416 | bytes 41943040 | tf_op jit(solution)/shard_map/bik,bic->bkc/dot_general | solution.py:63
  85.6 30.8 %reshape.66 = f32[32,2,128,6,128]{2,1,4,3,0:T(2,128)} reshape(f32[32,256,768]{1,2,0:T(8,128)} %fusion.14) | data formatting | bytes 50331648 | tf_op jit(solution)/shard_map/reshape | solution.py:66
  116.3 36.9 %copy.37 = f32[32,2,6,128,128]{4,3,2,1,0:T(8,128)} copy(f32[32,2,6,128,128]{3,1,4,2,0:T(2,128)} %bitcast.36) | data formatting | bytes 50331648 | tf_op jit(solution)/shard_map/transpose | solution.py:67
  153.6 52.5 %scatter_fusion = f32[4,12,128,128]{3,2,1,0:T(8,128)S(1)} fusion(f32[4,12,128,128]{3,2,1,0:T(8,128)S(1)} %broadcast_in_dim.35, s32[384]{0:T(512)S(1)} %reshape.75, f32[384,128,128]{2,1,0:T(8,128)} %bitcast.34), kind=kCustom, calls=%fused_computation.1 | custom fusion | flops 6291456 | bytes 75500544 | tf_op jit(solution)/shard_map/scatter-add | solution.py:97
  206.1 2.8 copy.38
  208.9 2.2 copy.46
  212.8 6.7 %all-to-all-start = ((f32[16,32,512]{2,1,0:T(8,128)}), f32[16,32,512]{2,1,0:T(8,128)S(1)}, u32[]{:S(2)}, u32[]{:S(2)}) async-start(f32[16,32,512]{2,1,0:T(8,128)} %bitcast.10), calls=%async_computation | async-start | bytes 2097152 | tf_op jit(solution)/shard_map/all_to_all | solution.py:109
  220.8 28.8 %all-to-all-done = f32[16,32,512]{2,1,0:T(8,128)S(1)} async-done(((f32[16,32,512]{2,1,0:T(8,128)}), f32[16,32,512]{2,1,0:T(8,128)S(1)}, u32[]{:S(2)}, u32[]{:S(2)}) %all-to-all-start) | async-done | bytes 1048608 | tf_op jit(solution)/shard_map/all_to_all | solution.py:109
  249.6 3.8 %all-to-all-start.1 = ((f32[16,32,512]{2,1,0:T(8,128)}), f32[16,32,512]{2,1,0:T(8,128)S(1)}, u32[]{:S(2)}, u32[]{:S(2)}) async-start(f32[16,32,512]{2,1,0:T(8,128)} %bitcast.12), calls=%async_computation.1 | async-start | bytes 2097152 | tf_op jit(solution)/shard_map/all_to_all | solution.py:47
  253.5 8.5 %gather_fusion = f32[512]{0:T(512)S(1)} fusion(f32[512,512]{1,0:T(8,128)} %copy.43, s32[512]{0:T(512)S(1)} %bitcast.39), kind=kCustom, calls=%fused_computation | custom fusion | bytes 8192 | tf_op jit(solution)/shard_map/jit(diagonal)/cond/branch_0_fun/gather | solution.py:99
  262.6 11.0 %psum.35 = f32[]{:T(128)} all-reduce(f32[]{:T(128)} %reduce_sum.19), channel_id=1, replica_groups=mesh['grp_0'=4,'grp_1'=2,'grp_2'=2,'dev_0'=4,'dev_1'=4] {'grp_0'}, use_global_device_ids=true, to_apply=%region_3.4 | all-reduce | flops 1 | bytes 8 | tf_op jit(solution)/shard_map/psum | solution.py:35
  273.6 5.5 %psum.36 = f32[]{:T(128)} all-reduce(f32[]{:T(128)} %psum.35), channel_id=1, replica_groups=mesh['grp_0'=4,'grp_1'=2,'grp_2'=2,'dev_0'=4,'dev_1'=4] {'grp_1'}, use_global_device_ids=true, to_apply=%region_4.5 | all-reduce | flops 1 | bytes 8 | tf_op jit(solution)/shard_map/psum | solution.py:35
  279.2 3.1 psum.37
  282.2 13.3 %psum.38 = f32[]{:T(128)} all-reduce(f32[]{:T(128)} %psum.37), channel_id=1, replica_groups=mesh['grp_0'=4,'grp_1'=2,'grp_2'=2,'dev_0'=4,'dev_1'=4] {'dev_0'}, use_global_device_ids=true, to_apply=%region_6.7 | all-reduce | flops 1 | bytes 8 | tf_op jit(solution)/shard_map/psum | solution.py:35
  295.5 11.0 %psum.39 = f32[]{:T(128)} all-reduce(f32[]{:T(128)} %psum.38), channel_id=1, replica_groups=mesh['grp_0'=4,'grp_1'=2,'grp_2'=2,'dev_0'=4,'dev_1'=4] {'dev_1'}, use_global_device_ids=true, to_apply=%region_7.8 | all-reduce | flops 1 | bytes 8 | tf_op jit(solution)/shard_map/psum | solution.py:35
  (33 shorter events, 11.3 us)
Async XLA Ops:
  0.8 17.3 %collective-permute-start = (s32[1,2]{0,1:T(2,128)S(1)}, s32[1,2]{0,1:T(2,128)S(1)}, u32[]{:S(2)}, u32[]{:S(2)}) collective-permute-start(s32[1,2]{0,1:T(2,128)S(1)} %get-tuple-element.18), channel_id=1, source_target_pairs={{0,1},{1,2},{2,3},{3,4},{4,5},{5,6},{6,7},{7,8},{8,9},{9,10},{10,1... | collective-permute-start | bytes 32 | tf_op jit(solution)/shard_map/ppermute | solution.py:21
  2.4 15.7 %collective-permute-start.1 = (s32[1,2]{0,1:T(2,128)S(1)}, s32[1,2]{0,1:T(2,128)S(1)}, u32[]{:S(2)}, u32[]{:S(2)}) collective-permute-start(s32[1,2]{0,1:T(2,128)S(1)} %get-tuple-element.19), channel_id=1, source_target_pairs={{1,0},{2,1},{3,2},{4,3},{5,4},{6,5},{7,6},{8,7},{9,8},{10,9},{11,1... | collective-permute-start | bytes 32 | tf_op jit(solution)/shard_map/ppermute | solution.py:22
  9.6 13.2 %collective-permute-start.2 = (f32[1,2,128,128]{3,2,1,0:T(8,128)S(1)}, f32[1,2,128,128]{3,2,1,0:T(8,128)S(1)}, u32[]{:S(2)}, u32[]{:S(2)}) collective-permute-start(f32[1,2,128,128]{3,2,1,0:T(8,128)S(1)} %get-tuple-element.8), channel_id=1, source_target_pairs={{0,1},{1,2},{2,3},{3,4},{4,5},{5,6},{6,7},{7,8},{8,9},{9,10},{10,1... | collective-permute-start | bytes 393224 | tf_op jit(solution)/shard_map/ppermute | solution.py:21
  9.7 13.1 %collective-permute-start.3 = (f32[1,2,128,128]{3,2,1,0:T(8,128)S(1)}, f32[1,2,128,128]{3,2,1,0:T(8,128)S(1)}, u32[]{:S(2)}, u32[]{:S(2)}) collective-permute-start(f32[1,2,128,128]{3,2,1,0:T(8,128)S(1)} %get-tuple-element.9), channel_id=1, source_target_pairs={{1,0},{2,1},{3,2},{4,3},{5,4},{6,5},{7,6},{8,7},{9,8},{10,9},{11,1... | collective-permute-start | bytes 393224 | tf_op jit(solution)/shard_map/ppermute | solution.py:22
  46.8 15.3 %copy-start = (f32[32,128,2,128]{1,3,2,0:T(8,128)S(1)}, f32[32,128,2,128]{1,3,2,0:T(8,128)}, u32[]{:S(2)}) copy-start(f32[32,128,2,128]{1,3,2,0:T(8,128)} %copy.31) | copy-start | bytes 12582916
  212.8 36.9 %all-to-all-start = ((f32[16,32,512]{2,1,0:T(8,128)}), f32[16,32,512]{2,1,0:T(8,128)S(1)}, u32[]{:S(2)}, u32[]{:S(2)}) async-start(f32[16,32,512]{2,1,0:T(8,128)} %bitcast.10), calls=%async_computation | async-start | bytes 2097152 | tf_op jit(solution)/shard_map/all_to_all | solution.py:109
  249.6 57.6 %all-to-all-start.1 = ((f32[16,32,512]{2,1,0:T(8,128)}), f32[16,32,512]{2,1,0:T(8,128)S(1)}, u32[]{:S(2)}, u32[]{:S(2)}) async-start(f32[16,32,512]{2,1,0:T(8,128)} %bitcast.12), calls=%async_computation.1 | async-start | bytes 2097152 | tf_op jit(solution)/shard_map/all_to_all | solution.py:47
where the time goes:
time: 311 us; the launch traced here: 308 us
  local copies, waits for them, and re-layouts  108 us (35%)
  other arithmetic  59.1 us (19%)
  blocking collectives  44 us (14%)
  matrix products  38.7 us (12%)
  waiting for transfers between devices  32.1 us (10%)
  starting transfers between devices  25.2 us (8%)
    scatter-add x1, other arithmetic, local(): partial_value.at[coarse_ids[:, :, None], col_tiles[:, None, :]]  52.5 us
    psum x5, blocking collectives, by_axis(): x = lax.psum(x, axis)  44 us
    transpose x1, local copies, waits for them, and re-layouts, coarse_tiles(): return jnp.transpose(left_prod, (0, 1, 3, 2, 4))  36.9 us
    reshape x1, local copies, waits for them, and re-layouts, coarse_tiles(): left_prod.reshape(block_count, slot_count, tile_size, 3 * slot_count, til...  30.8 us
    all_to_all x1, waiting for transfers between devices, local(): lax.all_to_all(edge_block, DEV, split_axis=0, concat_axis=0, tiled=True)  28.8 us
    dot_general x1, matrix products, coarse_tiles(): jnp.einsum('bik,bic->bkc', widened[1:-1], right_prod, precision=lax.Preci...  23.4 us
    slice x3, local copies, waits for them, and re-layouts, coarse_tiles(): stacked = jnp.stack([widened[:-2], widened[1:-1], widened[2:]], axis=1)  16 us
    dot_general x1, matrix products, coarse_tiles(): jnp.einsum('bnij,bnjk->bnik', own_a, stacked, precision=lax.Precision.HIG...  15.3 us
  transfers between devices with their start and end apart: 6, of which 2 were waited for; matrix products, arithmetic and copies ran while one was open for 5% of the time, Pallas kernels for 0%

commit v1 on v0

--- a/solution.py
+++ b/solution.py
@@ -32,7 +32,7 @@
 
 def by_axis(x, axes):
     for axis in axes:
-        x = lax.psum(x, axis)
+        x = jnp.sum(lax.all_gather(x, axis), axis=0)
     return x
 
 

time: 311 us -> 322 us (1.035)
  local copies, waits for them, and re-layouts: 108 us -> 119 us
    psum x5 -> x0, blocking collectives: 44 us -> none  [by_axis(): x = lax.psum(x, axis)]
    unnamed x0 -> x5, blocking collectives: none -> 40.8 us
    unnamed x4 -> x29, local copies, waits for them, and re-layouts: 3.57 us -> 14.1 us
  transfers between devices with their start and end apart: 6 -> 6, of which waited for: 2 -> 2; matrix products, arithmetic and copies ran while one was open for 5% -> 9% of each run, Pallas kernels for 0% -> 0%
where the time goes in v1:
time: 322 us; the launch traced here: 319 us
  local copies, waits for them, and re-layouts  119 us (37%)
  other arithmetic  62.2 us (19%)
  blocking collectives  40.8 us (13%)
  matrix products  38.7 us (12%)
  waiting for transfers between devices  32.1 us (10%)
  starting transfers between devices  25.3 us (8%)
    scatter-add x1, other arithmetic, local(): partial_value.at[coarse_ids[:, :, None], col_tiles[:, None, :]]  52.5 us
    unnamed x5, blocking collectives  40.8 us
    transpose x1, local copies, waits for them, and re-layouts, coarse_tiles(): return jnp.transpose(left_prod, (0, 1, 3, 2, 4))  36.9 us
    reshape x1, local copies, waits for them, and re-layouts, coarse_tiles(): left_prod.reshape(block_count, slot_count, tile_size, 3 * slot_count, til...  30.8 us
    all_to_all x1, waiting for transfers between devices, local(): lax.all_to_all(edge_block, DEV, split_axis=0, concat_axis=0, tiled=True)  28.8 us
    dot_general x1, matrix products, coarse_tiles(): jnp.einsum('bik,bic->bkc', widened[1:-1], right_prod, precision=lax.Preci...  23.4 us
    slice x3, local copies, waits for them, and re-layouts, coarse_tiles(): stacked = jnp.stack([widened[:-2], widened[1:-1], widened[2:]], axis=1)  16 us
    dot_general x1, matrix products, coarse_tiles(): jnp.einsum('bnij,bnjk->bnik', own_a, stacked, precision=lax.Precision.HIG...  15.3 us
  transfers between devices with their start and end apart: 6, of which 2 were waited for; matrix products, arithmetic and copies ran while one was open for 9% of the time, Pallas kernels for 0%

profile of v1, /device:TPU:32, one launch (start us, length us, event | category | flops | bytes accessed | tf_op | source)
XLA Modules:
  0.0 318.5 jit_solution(6943979599259169452)
XLA Ops:
  2.4 6.2 %collective-permute-start.1 = (s32[1,2]{0,1:T(2,128)S(1)}, s32[1,2]{0,1:T(2,128)S(1)}, u32[]{:S(2)}, u32[]{:S(2)}) collective-permute-start(s32[1,2]{0,1:T(2,128)S(1)} %get-tuple-element.19), channel_id=1, source_target_pairs={{1,0},{2,1},{3,2},{4,3},{5,4},{6,5},{7,6},{8,7},{9,8},{10,9},{11,1... | collective-permute-start | bytes 32 | tf_op jit(solution)/shard_map/ppermute | solution.py:22
  9.7 6.9 %collective-permute-start.3 = (f32[1,2,128,128]{3,2,1,0:T(8,128)S(1)}, f32[1,2,128,128]{3,2,1,0:T(8,128)S(1)}, u32[]{:S(2)}, u32[]{:S(2)}) collective-permute-start(f32[1,2,128,128]{3,2,1,0:T(8,128)S(1)} %get-tuple-element.9), channel_id=1, source_target_pairs={{1,0},{2,1},{3,2},{4,3},{5,4},{6,5},{7,6},{8,7},{9,8},{10,9},{11,1... | collective-permute-start | bytes 393224 | tf_op jit(solution)/shard_map/ppermute | solution.py:22
  19.5 3.2 %collective-permute-done.2 = f32[1,2,128,128]{3,2,1,0:T(8,128)S(1)} collective-permute-done((f32[1,2,128,128]{3,2,1,0:T(8,128)S(1)}, f32[1,2,128,128]{3,2,1,0:T(8,128)S(1)}, u32[]{:S(2)}, u32[]{:S(2)}) %collective-permute-start.2) | collective-permute-done | bytes 131104 | tf_op jit(solution)/shard_map/ppermute | solution.py:21
  22.8 2.5 maximum_bitcast_fusion
  25.3 4.7 %fusion.10 = (f32[32,128,2,128]{3,1,2,0:T(8,128)}, f32[32,128,2,128]{3,1,2,0:T(8,128)}, f32[32,128,2,128]{3,1,2,0:T(8,128)}) fusion(f32[34,128,2,128]{3,1,2,0:T(8,128)S(1)} %maximum_bitcast_fusion), kind=kLoop, calls=%fused_computation.33 | loop fusion | bytes 25165824 | tf_op jit(solution)/shard_map/slice | solution.py:58
  30.0 5.6 %copy.31 = f32[32,128,2,128]{1,3,2,0:T(8,128)} copy(f32[32,128,2,128]{3,1,2,0:T(8,128)} %get-tuple-element.7) | data formatting | bytes 8388608 | tf_op jit(solution)/shard_map/slice | solution.py:64
  35.6 5.6 %copy.32 = f32[32,128,2,128]{1,3,2,0:T(8,128)} copy(f32[32,128,2,128]{3,1,2,0:T(8,128)} %get-tuple-element.5) | data formatting | bytes 8388608 | tf_op jit(solution)/shard_map/slice | solution.py:58
  41.2 5.6 %copy.34 = f32[32,128,2,128]{1,3,2,0:T(8,128)} copy(f32[32,128,2,128]{3,1,2,0:T(8,128)} %get-tuple-element.6) | data formatting | bytes 8388608 | tf_op jit(solution)/shard_map/slice | solution.py:58
  46.8 15.3 %fusion = f32[32,3,256,128]{3,2,1,0:T(8,128)S(1)} fusion(f32[32,3,128,128]{3,2,1,0:T(8,128)} %param.3, f32[32,1,128,256]{2,3,1,0:T(8,128)} %bitcast.51, f32[32,1,128,256]{2,3,1,0:T(8,128)} %bitcast.47, f32[32,1,128,256]{2,3,1,0:T(8,128)} %bitcast.50), kind=kOutput, calls=%fused_computation.2 | convolution fusion | flops 4838129664 | bytes 31457280 | tf_op jit(solution)/shard_map/bnij,bnjk->bnik/dot_general | solution.py:59
  62.2 23.4 %fusion.14 = f32[32,256,768]{1,2,0:T(8,128)} fusion(f32[32,128,256]{1,2,0:T(8,128)S(1)} %bitcast.48, f32[32,128,768]{1,2,0:T(8,128)S(1)} %bitcast.45), kind=kOutput, calls=%fused_computation.37 | convolution fusion | flops 9663676416 | bytes 41943040 | tf_op jit(solution)/shard_map/bik,bic->bkc/dot_general | solution.py:63
  85.6 30.8 %reshape.66 = f32[32,2,128,6,128]{2,1,4,3,0:T(2,128)} reshape(f32[32,256,768]{1,2,0:T(8,128)} %fusion.14) | data formatting | bytes 50331648 | tf_op jit(solution)/shard_map/reshape | solution.py:66
  116.3 36.9 %copy.37 = f32[32,2,6,128,128]{4,3,2,1,0:T(8,128)} copy(f32[32,2,6,128,128]{3,1,4,2,0:T(2,128)} %bitcast.46) | data formatting | bytes 50331648 | tf_op jit(solution)/shard_map/transpose | solution.py:67
  153.6 52.5 %scatter_fusion = f32[4,12,128,128]{3,2,1,0:T(8,128)S(1)} fusion(f32[4,12,128,128]{3,2,1,0:T(8,128)S(1)} %broadcast_in_dim.35, s32[384]{0:T(512)S(1)} %reshape.75, f32[384,128,128]{2,1,0:T(8,128)} %bitcast.44), kind=kCustom, calls=%fused_computation.1 | custom fusion | flops 6291456 | bytes 75500544 | tf_op jit(solution)/shard_map/scatter-add | solution.py:97
  206.1 2.8 copy.38
  208.9 2.2 copy.46
  212.8 6.8 %all-to-all-start = ((f32[16,32,512]{2,1,0:T(8,128)}), f32[16,32,512]{2,1,0:T(8,128)S(1)}, u32[]{:S(2)}, u32[]{:S(2)}) async-start(f32[16,32,512]{2,1,0:T(8,128)} %bitcast.10), calls=%async_computation | async-start | bytes 2097152 | tf_op jit(solution)/shard_map/all_to_all | solution.py:109
  221.0 28.8 %all-to-all-done = f32[16,32,512]{2,1,0:T(8,128)S(1)} async-done(((f32[16,32,512]{2,1,0:T(8,128)}), f32[16,32,512]{2,1,0:T(8,128)S(1)}, u32[]{:S(2)}, u32[]{:S(2)}) %all-to-all-start) | async-done | bytes 1048608 | tf_op jit(solution)/shard_map/all_to_all | solution.py:109
  249.8 3.8 %all-to-all-start.1 = ((f32[16,32,512]{2,1,0:T(8,128)}), f32[16,32,512]{2,1,0:T(8,128)S(1)}, u32[]{:S(2)}, u32[]{:S(2)}) async-start(f32[16,32,512]{2,1,0:T(8,128)} %bitcast.12), calls=%async_computation.1 | async-start | bytes 2097152 | tf_op jit(solution)/shard_map/all_to_all | solution.py:47
  254.3 8.4 %gather_fusion = f32[512]{0:T(512)S(1)} fusion(f32[512,512]{1,0:T(8,128)} %copy.43, s32[512]{0:T(512)S(1)} %bitcast.49), kind=kCustom, calls=%fused_computation | custom fusion | bytes 8192 | tf_op jit(solution)/shard_map/jit(diagonal)/cond/branch_0_fun/gather | solution.py:99
  265.5 10.4 %all-reduce = f32[4]{0:T(128)S(1)} all-reduce(f32[4]{0:T(128)S(1)} %dynamic-update-slice), channel_id=1, replica_groups=mesh['grp_0'=4,'grp_1'=2,'grp_2'=2,'dev_0'=4,'dev_1'=4] {'grp_0'}, use_global_device_ids=true, to_apply=%add | all-reduce | flops 4 | bytes 32
  278.6 4.9 %all-reduce.1 = f32[2]{0:T(128)S(1)} all-reduce(f32[2]{0:T(128)S(1)} %dynamic-update-slice.1), channel_id=1, replica_groups=mesh['grp_0'=4,'grp_1'=2,'grp_2'=2,'dev_0'=4,'dev_1'=4] {'grp_1'}, use_global_device_ids=true, to_apply=%add.1 | all-reduce | flops 2 | bytes 16
  286.2 2.4 all-reduce.2
  291.4 12.6 %all-reduce.3 = f32[4]{0:T(128)S(1)} all-reduce(f32[4]{0:T(128)S(1)} %dynamic-update-slice.3), channel_id=1, replica_groups=mesh['grp_0'=4,'grp_1'=2,'grp_2'=2,'dev_0'=4,'dev_1'=4] {'dev_0'}, use_global_device_ids=true, to_apply=%add.3 | all-reduce | flops 4 | bytes 32
  306.1 10.4 %all-reduce.4 = f32[4]{0:T(128)S(1)} all-reduce(f32[4]{0:T(128)S(1)} %dynamic-update-slice.4), channel_id=1, replica_groups=mesh['grp_0'=4,'grp_1'=2,'grp_2'=2,'dev_0'=4,'dev_1'=4] {'dev_1'}, use_global_device_ids=true, to_apply=%add.4 | all-reduce | flops 4 | bytes 32
  (63 shorter events, 24.8 us)
Async XLA Ops:
  0.8 17.3 %collective-permute-start = (s32[1,2]{0,1:T(2,128)S(1)}, s32[1,2]{0,1:T(2,128)S(1)}, u32[]{:S(2)}, u32[]{:S(2)}) collective-permute-start(s32[1,2]{0,1:T(2,128)S(1)} %get-tuple-element.18), channel_id=1, source_target_pairs={{0,1},{1,2},{2,3},{3,4},{4,5},{5,6},{6,7},{7,8},{8,9},{9,10},{10,1... | collective-permute-start | bytes 32 | tf_op jit(solution)/shard_map/ppermute | solution.py:21
  2.4 15.7 %collective-permute-start.1 = (s32[1,2]{0,1:T(2,128)S(1)}, s32[1,2]{0,1:T(2,128)S(1)}, u32[]{:S(2)}, u32[]{:S(2)}) collective-permute-start(s32[1,2]{0,1:T(2,128)S(1)} %get-tuple-element.19), channel_id=1, source_target_pairs={{1,0},{2,1},{3,2},{4,3},{5,4},{6,5},{7,6},{8,7},{9,8},{10,9},{11,1... | collective-permute-start | bytes 32 | tf_op jit(solution)/shard_map/ppermute | solution.py:22
  9.6 13.2 %collective-permute-start.2 = (f32[1,2,128,128]{3,2,1,0:T(8,128)S(1)}, f32[1,2,128,128]{3,2,1,0:T(8,128)S(1)}, u32[]{:S(2)}, u32[]{:S(2)}) collective-permute-start(f32[1,2,128,128]{3,2,1,0:T(8,128)S(1)} %get-tuple-element.8), channel_id=1, source_target_pairs={{0,1},{1,2},{2,3},{3,4},{4,5},{5,6},{6,7},{7,8},{8,9},{9,10},{10,1... | collective-permute-start | bytes 393224 | tf_op jit(solution)/shard_map/ppermute | solution.py:21
  9.7 13.1 %collective-permute-start.3 = (f32[1,2,128,128]{3,2,1,0:T(8,128)S(1)}, f32[1,2,128,128]{3,2,1,0:T(8,128)S(1)}, u32[]{:S(2)}, u32[]{:S(2)}) collective-permute-start(f32[1,2,128,128]{3,2,1,0:T(8,128)S(1)} %get-tuple-element.9), channel_id=1, source_target_pairs={{1,0},{2,1},{3,2},{4,3},{5,4},{6,5},{7,6},{8,7},{9,8},{10,9},{11,1... | collective-permute-start | bytes 393224 | tf_op jit(solution)/shard_map/ppermute | solution.py:22
  46.8 15.3 %copy-start = (f32[32,128,2,128]{1,3,2,0:T(8,128)S(1)}, f32[32,128,2,128]{1,3,2,0:T(8,128)}, u32[]{:S(2)}) copy-start(f32[32,128,2,128]{1,3,2,0:T(8,128)} %copy.31) | copy-start | bytes 12582916
  211.4 42.2 %copy-start.5 = (u32[256]{0:T(256)S(1)}, u32[256]{0:T(256)}, u32[]{:S(2)}) copy-start(u32[256]{0:T(256)} %constant.72) | copy-start | bytes 3076
  212.8 52.0 %copy-start.4 = (u32[256]{0:T(256)S(1)}, u32[256]{0:T(256)}, u32[]{:S(2)}) copy-start(u32[256]{0:T(256)} %constant.77) | copy-start | bytes 3076
  212.8 65.1 %copy-start.3 = (u32[256]{0:T(256)S(1)}, u32[256]{0:T(256)}, u32[]{:S(2)}) copy-start(u32[256]{0:T(256)} %constant.82) | copy-start | bytes 3076
  212.8 72.7 %copy-start.2 = (u32[256]{0:T(256)S(1)}, u32[256]{0:T(256)}, u32[]{:S(2)}) copy-start(u32[256]{0:T(256)} %constant.87) | copy-start | bytes 3076
  212.8 77.9 %copy-start.1 = (u32[256]{0:T(256)S(1)}, u32[256]{0:T(256)}, u32[]{:S(2)}) copy-start(u32[256]{0:T(256)} %constant.92) | copy-start | bytes 3076
  212.8 37.0 %all-to-all-start = ((f32[16,32,512]{2,1,0:T(8,128)}), f32[16,32,512]{2,1,0:T(8,128)S(1)}, u32[]{:S(2)}, u32[]{:S(2)}) async-start(f32[16,32,512]{2,1,0:T(8,128)} %bitcast.10), calls=%async_computation | async-start | bytes 2097152 | tf_op jit(solution)/shard_map/all_to_all | solution.py:109
  249.8 67.9 %all-to-all-start.1 = ((f32[16,32,512]{2,1,0:T(8,128)}), f32[16,32,512]{2,1,0:T(8,128)S(1)}, u32[]{:S(2)}, u32[]{:S(2)}) async-start(f32[16,32,512]{2,1,0:T(8,128)} %bitcast.12), calls=%async_computation.1 | async-start | bytes 2097152 | tf_op jit(solution)/shard_map/all_to_all | solution.py:47
